TPU v7x, 32 devices: a whole 2x2x4 slice. The times are simulated.
32 devices in a mesh: expert: 4 (over z), tensor: 8 (over y, x, core).
Axes of the slice: x: 2, y: 2, z: 4, core: 2. Of those that a mesh axis runs over, the one named last changes fastest.
Arguments:
- stashed: bfloat16 [384, 4096], P('expert', 'tensor'), may hold values from -6 to 6
- expert_ids: int32 [384, 2], P('expert'), may hold values from 0 to 3, all different within a row; in each aligned block of 96 rows (0 to 95, 96 to 191, ...) at most 64 rows name the same one
- combine_weight: float32 [384, 2], P('expert'), may hold values from 0.2 to 1
- w_gate: bfloat16 [4, 7168, 4096], P('expert', 'tensor'), may hold values from -0.09375 to 0.09375
- w_up: bfloat16 [4, 7168, 4096], P('expert', 'tensor'), may hold values from -0.09375 to 0.09375
- w_down: bfloat16 [4, 7168, 4096], P('expert', 'tensor'), may hold values from -0.09375 to 0.09375
Outputs:
- mixed_out: bfloat16 [384, 4096], P('expert', 'tensor')
Inputs may be any that keep to these rules, and one draw needn't show every extreme that they name: `expert_ids`: each row names two different experts. Among the 96 rows of one group (aligned blocks) no expert is named more than 64 times, and in some group some expert is named exactly 64 times.
All inputs are finite; a program needn't handle non-finite values.
Results may differ from a plain program's by a relative error of at most 0.0049.
Values may be sent and summed in bfloat16 or wider, within the bound.
A program may use at most 64 MiB of HBM per device.

v0:
```python
import jax
import jax.numpy as jnp
from jax import lax
from jax.sharding import PartitionSpec as P


def slot_targets(expert_ids, experts, capacity):
    flat_ids = expert_ids.reshape(-1)
    one_hot = (flat_ids[:, None] == jnp.arange(experts, dtype=jnp.int32)[None, :]).astype(jnp.int32)
    before = jnp.cumsum(one_hot, axis=0) - one_hot
    slot_index = jnp.sum(before * one_hot, axis=1)
    return (flat_ids * capacity + slot_index).reshape(expert_ids.shape)


def contract_last(left, right):
    return lax.dot_general(
        left, right, (((1,), (1,)), ((), ())), preferred_element_type=jnp.float32
    )


def shards(stashed, expert_ids, combine_weight, w_gate, w_up, w_down):
    tok_count = stashed.shape[0]
    feat_width = stashed.shape[1]
    experts = lax.axis_size("expert")
    capacity = min(tok_count, 8 * tok_count // (3 * experts))
    targets = slot_targets(expert_ids, experts, capacity)
    columns = jnp.arange(experts * capacity, dtype=jnp.int32)
    pair_match = (targets[:, :, None] == columns[None, None, :]).astype(jnp.float32)
    selector = jnp.sum(pair_match, axis=1).T.astype(jnp.bfloat16)
    mixing = jnp.sum(pair_match * combine_weight[:, :, None], axis=1)
    gate_w = w_gate[0]
    up_w = w_up[0]
    down_w = w_down[0]
    gathered = lax.all_gather(stashed, "tensor", axis=1, tiled=True)
    outgoing = jnp.dot(selector, gathered, preferred_element_type=jnp.float32).astype(jnp.bfloat16)
    outgoing = outgoing.reshape(experts, capacity, gathered.shape[1])
    received = lax.all_to_all(outgoing, "expert", split_axis=0, concat_axis=0, tiled=True)
    sources, item_count, full_width = received.shape
    rows_in = received.reshape(sources * item_count, full_width)
    gate_acts = contract_last(rows_in, gate_w)
    up_acts = contract_last(rows_in, up_w)
    hidden = (jax.nn.silu(gate_acts) * up_acts).astype(jnp.bfloat16)
    result = jnp.dot(hidden, down_w, preferred_element_type=jnp.float32)
    partial_value = result.reshape(sources, item_count, result.shape[1])
    partial_value = partial_value.reshape(-1, partial_value.shape[2])
    own_share = lax.psum_scatter(partial_value, "tensor", scatter_dimension=1, tiled=True)
    returned_rows = lax.all_to_all(
        own_share.reshape(experts, capacity, feat_width),
        "expert",
        split_axis=0,
        concat_axis=0,
        tiled=True,
    )
    combined = jnp.dot(
        mixing,
        returned_rows.reshape(experts * capacity, feat_width),
        precision=lax.Precision.HIGHEST,
        preferred_element_type=jnp.float32,
    )
    return combined.astype(jnp.bfloat16)


def solution(mesh):
    return jax.shard_map(
        shards,
        mesh=mesh,
        in_specs=(
            P("expert", "tensor"),
            P("expert", None),
            P("expert", None),
            P("expert", "tensor", None),
            P("expert", "tensor", None),
            P("expert", "tensor", None),
        ),
        out_specs=P("expert", "tensor"),
        check_vma=False,
    )
```

profile of v0, /device:TPU:0, one launch (start us, length us, event | category | flops | bytes accessed | tf_op | source)
XLA Modules:
  0.0 167.9 jit_solution(18047453095320567481)
XLA Ops:
  6.5 0.0 reduce-scatter.2.cloned.1.call-start
  6.5 0.8 copy.23
  7.3 0.1 eq.35
  7.5 1.2 reduce-window.6
  8.7 0.1 slice.12
  8.8 0.1 copy.24
  8.9 0.1 copy.25
  9.0 0.1 add_bitcast_fusion
  9.1 0.1 reduce_sum.30
  9.3 0.1 copy.26
  9.3 0.0 copy-start
  9.3 0.9 multiply_add_fusion
  10.2 12.5 %all_gather.3 = bf16[96,4096]{1,0:T(8,128)(2,1)S(1)} all-gather(bf16[96,512]{1,0:T(8,128)(2,1)} %param.6), channel_id=1, replica_groups=mesh['expert'=4,'tensor'=8] {'tensor'}, dimensions={1}, use_global_device_ids=true | all-gather | bytes 884736 | tf_op jit(solution)/shard_map/all_gather | solution.py:34
  22.7 0.8 convert_reduce_fusion
  23.5 0.7 convolution_convert_fusion
  24.2 53.4 %all_to_all.10 = bf16[4,64,4096]{2,1,0:T(8,128)(2,1)S(1)} all-to-all(bf16[4,64,4096]{2,1,0:T(8,128)(2,1)S(1)} %bitcast.34), channel_id=1, replica_groups=mesh['expert'=4,'tensor'=8] {'expert'}, dimensions={0} | all-to-all | bytes 4194304 | tf_op jit(solution)/shard_map/all_to_all | solution.py:37
  77.6 0.0 copy-done
  77.6 2.4 %fusion.4 = f32[256,896]{1,0:T(8,128)S(1)} fusion(bf16[256,4096]{1,0:T(8,128)(2,1)S(1)} %bitcast.35, bf16[1,896,4096]{2,1,0:T(8,128)(2,1)S(1)} %copy-done), kind=kOutput, calls=%fused_computation.4 | convolution fusion | flops 1879048192 | bytes 10354688 | tf_op jit(solution)/shard_map/dot_general | solution.py:16
  80.0 11.7 %fusion = f32[256,4096]{1,0:T(8,128)} fusion(bf16[1,896,4096]{2,1,0:T(8,128)(2,1)} %param.11, bf16[256,4096]{1,0:T(8,128)(2,1)S(1)} %bitcast.36, bf16[1,896,4096]{2,1,0:T(8,128)(2,1)} %param.10, f32[256,896]{1,0:T(8,128)S(1)} %fusion.4), kind=kOutput, calls=%fused_computation | convolution fusion | flops 3759472640 | bytes 21889024 | tf_op jit(solution)/shard_map/dot_general | solution.py:43
  91.7 0.0 reduce-scatter.2.cloned.1.call-update
  91.7 49.4 %reduce-scatter.2.cloned.1.call-done = f32[256,512]{1,0:T(8,128)} async-done(((f32[256,4096]{1,0:T(8,128)}), f32[256,512]{1,0:T(8,128)}) %reduce-scatter.2.cloned.1.call-update) | async-done | bytes 524304 | tf_op jit(solution)/shard_map/reduce_scatter | solution.py:46
  141.1 18.9 %all_to_all.11 = f32[4,64,512]{2,1,0:T(8,128)S(1)} all-to-all(f32[4,64,512]{2,1,0:T(8,128)} %bitcast.38), channel_id=1, replica_groups=mesh['expert'=4,'tensor'=8] {'expert'}, dimensions={0} | all-to-all | bytes 1048576 | tf_op jit(solution)/shard_map/all_to_all | solution.py:47
  160.0 1.1 convolution_convert_fusion.1
  (7 shorter events, 0.1 us)
Async XLA Ops:
  6.5 134.6 %reduce-scatter.2.cloned.1.call-start = ((), (), s32[]{:S(2)}) async-start(), calls=%async_computation.3 | async-start | bytes 4718592 | tf_op jit(solution)/shard_map/reduce_scatter | solution.py:46
  9.3 68.3 %copy-start = (bf16[1,896,4096]{2,1,0:T(8,128)(2,1)S(1)}, bf16[1,896,4096]{2,1,0:T(8,128)(2,1)}, u32[]{:S(2)}) copy-start(bf16[1,896,4096]{2,1,0:T(8,128)(2,1)} %param.9) | copy-start | bytes 22020100
Sparse Core Ops, SparseCore 0:
  91.8 49.2 reduce-scatter.1
where the time goes:
time: 168 us
  blocking collectives  84.8 us (50%)
  waiting for transfers between devices  49.4 us (29%)
  matrix products  15.9 us (9%)
  between operations  13.4 us (8%)
  other arithmetic  3.03 us (2%)
    all_to_all x1, blocking collectives, shards(): lax.all_to_all(outgoing, 'expert', split_axis=0, concat_axis=0, tiled=True)  53.4 us
    reduce_scatter x1, waiting for transfers between devices, shards(): lax.psum_scatter(partial_value, 'tensor', scatter_dimension=1, tiled=True)  49.4 us
    all_to_all x1, blocking collectives, shards(): lax.all_to_all(own_share.reshape(experts, capacity, feat_width), 'expert'...  18.9 us
    all_gather x1, blocking collectives, shards(): gathered = lax.all_gather(stashed, 'tensor', axis=1, tiled=True)  12.5 us
    dot_general x1, matrix products, shards(): result = jnp.dot(hidden, down_w, preferred_element_type=jnp.float32)  11.7 us
  transfers between devices with their start and end apart: 1, of which 1 were waited for; matrix products, arithmetic and copies ran while one was open for 0% of the time, Pallas kernels for 0%

commit v1 on v0

--- a/solution.py
+++ b/solution.py
@@ -1,6 +1,10 @@
+import functools
+
 import jax
 import jax.numpy as jnp
 from jax import lax
+from jax.experimental import pallas as pl
+from jax.experimental.pallas import tpu as pltpu
 from jax.sharding import PartitionSpec as P
 
 
@@ -60,9 +64,297 @@
     return combined.astype(jnp.bfloat16)
 
 
+MESH = pl.DeviceIdType.MESH
+
+
+def flip(index, bit):
+    return index + bit - 2 * bit * lax.rem(lax.div(index, bit), 2)
+
+
+def layer_kernel(
+    groups, cap,
+    x_ref, ids_ref, cw_ref, wg_hbm, wu_hbm, wd_hbm, out_ref,
+    wg, wu, wd, picked, rows_in, gate_acc, up_acc, hidden,
+    sib_out, sib_in, own_part, d_out, d_in, x_out, x_in, y_out, y_in, z_out, z_in,
+    w_sem, send_sem, recv_sem,
+):
+    tokens, feat = x_ref.shape
+    z = lax.axis_index("expert")
+    t = lax.axis_index("tensor")
+    sib, tx, ty = flip(t, 1), flip(t, 2), flip(t, 4)
+    td = flip(tx, 4)
+    group_of = [z, flip(z, 1), flip(z, 2), flip(flip(z, 1), 2)]
+    steps = range(groups)
+
+    loads = []
+    for i, (hbm, vmem) in enumerate(((wg_hbm, wg), (wu_hbm, wu), (wd_hbm, wd))):
+        half = vmem.shape[0] // 2
+        for j in range(2):
+            part = pl.ds(j * half, half)
+            loads.append(pltpu.make_async_copy(hbm.at[0, part], vmem.at[part], w_sem.at[2 * i + j]))
+    for load in loads:
+        load.start()
+
+    barrier = pltpu.get_barrier_semaphore()
+    peers = [{"tensor": sib}, {"tensor": tx}, {"tensor": ty}]
+    peers += [{"expert": group_of[s]} for s in steps[1:]]
+    for peer in peers:
+        pl.semaphore_signal(barrier, inc=1, device_id=peer, device_id_type=MESH)
+
+    ids = ids_ref[...]
+    lanes = lax.broadcasted_iota(jnp.int32, (tokens, 128), 1)
+    first = (ids[:, 0:1] == lanes).astype(jnp.float32)
+    second = (ids[:, 1:2] == lanes).astype(jnp.float32)
+    earlier = (
+        lax.broadcasted_iota(jnp.int32, (tokens, tokens), 1)
+        < lax.broadcasted_iota(jnp.int32, (tokens, tokens), 0)
+    ).astype(jnp.bfloat16)
+    before = jnp.dot(earlier, (first + second).astype(jnp.bfloat16), preferred_element_type=jnp.float32)
+    slot0 = jnp.sum(before * first, axis=1, keepdims=True)
+    slot1 = jnp.sum((before + first) * second, axis=1, keepdims=True)
+    place = (ids ^ z).astype(jnp.float32) * cap
+    columns = lax.broadcasted_iota(jnp.int32, (tokens, groups * cap), 1).astype(jnp.float32)
+    match0 = (columns == place[:, 0:1] + slot0).astype(jnp.float32)
+    match1 = (columns == place[:, 1:2] + slot1).astype(jnp.float32)
+    selector = (match0 + match1).astype(jnp.bfloat16)
+    picked[...] = lax.dot_general(
+        selector, x_ref[...], (((0,), (0,)), ((), ())), preferred_element_type=jnp.float32
+    ).astype(jnp.bfloat16)
+
+    def group_rows(s):
+        return pl.ds(pl.multiple_of(group_of[s] * cap, cap), cap)
+
+    def block(owner, s):
+        lanes_at = pl.ds(pl.multiple_of(lax.rem(owner, 2) * feat, feat), feat)
+        return rows_in.at[lax.div(owner, 2), group_rows(s), lanes_at]
+
+    copies = {}
+
+    def send(name, s, src, dst, peer):
+        number = NAMES.index(name) * groups + s
+        copy = pltpu.make_async_remote_copy(
+            src_ref=src, dst_ref=dst, send_sem=send_sem.at[number], recv_sem=recv_sem.at[number],
+            device_id=peer, device_id_type=MESH,
+        )
+        copy.start()
+        copies[name, s] = copy
+
+    def arrive(name, s):
+        copies[name, s].wait_recv()
+
+    own_at = block(t, 0)
+    own_at[...] = picked[pl.ds(0, cap)]
+    pl.semaphore_wait(barrier, len(peers))
+
+    def share(s):
+        here = block(t, s)
+        send("own_x", s, here, here, {"tensor": tx})
+        send("own_y", s, here, here, {"tensor": ty})
+        send("own_sib", s, here, here, {"tensor": sib})
+
+    def pass_x(s):
+        arrive("own_x", s)
+        here = block(tx, s)
+        if s % 2 == 0:
+            send("diag", s, here, here, {"tensor": ty})
+        send("sib_x", s, here, here, {"tensor": sib})
+
+    def pass_y(s):
+        arrive("own_y", s)
+        here = block(ty, s)
+        if s % 2 == 1:
+            send("diag", s, here, here, {"tensor": tx})
+        send("sib_y", s, here, here, {"tensor": sib})
+
+    def pass_diag(s):
+        arrive("diag", s)
+        here = block(td, s)
+        send("sib_d", s, here, here, {"tensor": sib})
+
+    def project(owner, start):
+        pair = lax.div(owner, 2)
+        rows = rows_in[pair]
+        lanes_at = pl.ds(pl.multiple_of(pair * (2 * feat), 2 * feat), 2 * feat)
+        for weight, acc in ((wg, gate_acc), (wu, up_acc)):
+            part = contract_last(rows, weight[:, lanes_at])
+            acc[...] = part if start else acc[...] + part
+
+    for s in (3, 2, 1):
+        send("z", s, picked.at[pl.ds(s * cap, cap)], block(t, 0), {"expert": group_of[s]})
+    share(0)
+    arrive("z", 1)
+    share(1)
+    pass_x(0)
+    pass_y(0)
+    arrive("z", 2)
+    share(2)
+    arrive("z", 3)
+    share(3)
+    pass_x(1)
+    pass_y(1)
+    for load in loads[:4]:
+        load.wait()
+    for s in steps:
+        arrive("own_sib", s)
+    project(t, True)
+    pass_x(2)
+    pass_y(2)
+    pass_diag(0)
+    pass_diag(1)
+    pass_x(3)
+    pass_y(3)
+    for s in steps:
+        arrive("sib_x", s)
+    project(tx, False)
+    pass_diag(2)
+    pass_diag(3)
+    for s in steps:
+        arrive("sib_y", s)
+    project(ty, False)
+    for s in steps:
+        arrive("sib_d", s)
+    project(td, False)
+    gate = gate_acc[...]
+    hidden[...] = (gate / (1.0 + jnp.exp(-gate)) * up_acc[...]).astype(jnp.bfloat16)
+    for load in loads[4:]:
+        load.wait()
+
+    owners = (t, tx, ty, td)
+
+    def down(owner):
+        lanes_at = pl.ds(pl.multiple_of(owner * feat, feat), feat)
+        return jnp.dot(hidden[...], wd[:, lanes_at], preferred_element_type=jnp.float32)
+
+    def partial_sums(q):
+        sib_out[q] = down(flip(owners[q], 1)).astype(jnp.bfloat16)
+        send("sum_sib", q, sib_out.at[q], sib_in.at[q], {"tensor": sib})
+        own_part[q] = down(owners[q])
+
+    def chip_sum(q, s):
+        at = group_rows(s)
+        return own_part[q, at] + sib_in[q, at].astype(jnp.float32)
+
+    def sum_d(s):
+        d_out[s] = chip_sum(3, s).astype(jnp.bfloat16)
+        send("sum_d", s, d_out.at[s], d_in.at[s], {"tensor": tx if s % 2 == 0 else ty})
+
+    def sum_x(s):
+        value = chip_sum(1, s)
+        if s % 2 == 1:
+            arrive("sum_d", s)
+            value = value + d_in[s].astype(jnp.float32)
+        x_out[s] = value.astype(jnp.bfloat16)
+        send("sum_x", s, x_out.at[s], x_in.at[s], {"tensor": tx})
+
+    def sum_y(s):
+        value = chip_sum(2, s)
+        if s % 2 == 0:
+            arrive("sum_d", s)
+            value = value + d_in[s].astype(jnp.float32)
+        y_out[s] = value.astype(jnp.bfloat16)
+        send("sum_y", s, y_out.at[s], y_in.at[s], {"tensor": ty})
+
+    def total(s):
+        arrive("sum_x", s)
+        arrive("sum_y", s)
+        value = chip_sum(0, s) + x_in[s].astype(jnp.float32) + y_in[s].astype(jnp.float32)
+        return value.astype(jnp.bfloat16)
+
+    def give_back(s):
+        z_out[s] = total(s)
+        send("back", s, z_out.at[s], z_in.at[pl.ds(s * cap, cap)], {"expert": group_of[s]})
+
+    partial_sums(3)
+    partial_sums(1)
+    arrive("sum_sib", 3)
+    sum_d(2)
+    sum_d(3)
+    partial_sums(2)
+    arrive("sum_sib", 1)
+    sum_x(2)
+    arrive("sum_sib", 2)
+    sum_y(3)
+    sum_d(0)
+    sum_d(1)
+    partial_sums(0)
+    sum_x(3)
+    sum_y(2)
+    sum_x(0)
+    sum_y(1)
+    arrive("sum_sib", 0)
+    give_back(2)
+    give_back(3)
+    sum_x(1)
+    sum_y(0)
+    give_back(1)
+    z_in[pl.ds(0, cap)] = total(0)
+
+    weights = cw_ref[...]
+    mixing = match0 * weights[:, 0:1] + match1 * weights[:, 1:2]
+    coarse = mixing.astype(jnp.bfloat16)
+    fine = (mixing - coarse.astype(jnp.float32)).astype(jnp.bfloat16)
+    for s in (2, 3, 1):
+        arrive("back", s)
+    returned = z_in[...]
+    combined = jnp.dot(coarse, returned, preferred_element_type=jnp.float32)
+    combined += jnp.dot(fine, returned, preferred_element_type=jnp.float32)
+    out_ref[...] = combined.astype(jnp.bfloat16)
+    for copy in copies.values():
+        copy.wait_send()
+
+
+NAMES = (
+    "z", "own_x", "own_y", "own_sib", "diag", "sib_x", "sib_y", "sib_d",
+    "sum_sib", "sum_d", "sum_x", "sum_y", "back",
+)
+
+
+def fused_shards(stashed, expert_ids, combine_weight, w_gate, w_up, w_down):
+    groups = lax.axis_size("expert")
+    tokens, feat = stashed.shape
+    cap = min(tokens, 8 * tokens // (3 * groups))
+    _, units, width = w_gate.shape
+    rows = groups * cap
+    bf16, f32 = jnp.bfloat16, jnp.float32
+    vmem = pl.BlockSpec(memory_space=pltpu.VMEM)
+    hbm = pl.BlockSpec(memory_space=pl.ANY)
+    pieces = [pltpu.VMEM((groups, cap, feat), bf16)] * 7
+    return pl.pallas_call(
+        functools.partial(layer_kernel, groups, cap),
+        out_shape=jax.ShapeDtypeStruct((tokens, feat), bf16),
+        in_specs=[vmem, vmem, vmem, hbm, hbm, hbm],
+        out_specs=vmem,
+        scratch_shapes=[
+            pltpu.VMEM((units, width), bf16),
+            pltpu.VMEM((units, width), bf16),
+            pltpu.VMEM((units, width), bf16),
+            pltpu.VMEM((rows, feat), bf16),
+            pltpu.VMEM((width // (2 * feat), rows, 2 * feat), bf16),
+            pltpu.VMEM((rows, units), f32),
+            pltpu.VMEM((rows, units), f32),
+            pltpu.VMEM((rows, units), bf16),
+            pltpu.VMEM((4, rows, feat), bf16),
+            pltpu.VMEM((4, rows, feat), bf16),
+            pltpu.VMEM((4, rows, feat), f32),
+            *pieces,
+            pltpu.VMEM((rows, feat), bf16),
+            pltpu.SemaphoreType.DMA((6,)),
+            pltpu.SemaphoreType.DMA((len(NAMES) * groups,)),
+            pltpu.SemaphoreType.DMA((len(NAMES) * groups,)),
+        ],
+        compiler_params=pltpu.CompilerParams(
+            collective_id=0, has_side_effects=True, vmem_limit_bytes=60 * 1024 * 1024
+        ),
+    )(stashed, expert_ids, combine_weight, w_gate, w_up, w_down)
+
+
+def picks_kernel(mesh):
+    return mesh.shape["tensor"] == 8 and mesh.shape["expert"] == 4
+
+
 def solution(mesh):
     return jax.shard_map(
-        shards,
+        fused_shards if picks_kernel(mesh) else shards,
         mesh=mesh,
         in_specs=(
             P("expert", "tensor"),

time: 168 us -> 48.6 us (0.29)
  blocking collectives: 84.8 us -> 0 us
  waiting for transfers between devices: 49.4 us -> 0 us
  Pallas kernels: 0 us -> 44.1 us
  matrix products: 15.9 us -> 0 us
  between operations: 13.4 us -> 0.01 us
  other arithmetic: 3.03 us -> 0 us
  local copies, waits for them, and re-layouts: 1.42 us -> 4.32 us
    all_to_all x2 -> x0, blocking collectives: 72.3 us -> none  [the longest x1 53.4 us: shards(): lax.all_to_all(outgoing, 'expert', split_axis=0, concat_axis=0, tiled=True)]
    reduce_scatter x1 -> x0, waiting for transfers between devices: 49.4 us -> none  [shards(): lax.psum_scatter(partial_value, 'tensor', scatter_dimension=1, tiled=True)]
    pallas_call x0 -> x1, Pallas kernels: none -> 44.1 us  [fused_shards(): pl.pallas_call(functools.partial(layer_kernel, groups, cap), out_shape=ja...]
    dot_general x4 -> x0, matrix products: 15.9 us -> none  [the longest x1 11.7 us: shards(): result = jnp.dot(hidden, down_w, preferred_element_type=jnp.float32)]
    all_gather x1 -> x0, blocking collectives: 12.5 us -> none  [shards(): gathered = lax.all_gather(stashed, 'tensor', axis=1, tiled=True)]
    unnamed x4 -> x3, local copies, waits for them, and re-layouts: 0.78 us -> 4.32 us
  transfers between devices with their start and end apart: 1 -> 0, of which waited for: 1 -> 0; matrix products, arithmetic and copies ran while one was open for 0% -> 0% of each run, Pallas kernels for 0% -> 0%
where the time goes in v1:
time: 48.6 us; the launch traced here: 48.4 us
  Pallas kernels  44.1 us (91%)
  local copies, waits for them, and re-layouts  4.32 us (9%)
    pallas_call x1, Pallas kernels, fused_shards(): pl.pallas_call(functools.partial(layer_kernel, groups, cap), out_shape=ja...  44.1 us
    unnamed x3, local copies, waits for them, and re-layouts  4.32 us

profile of v1, /device:TPU:0, one launch (start us, length us, event | category | flops | bytes accessed | tf_op | source)
XLA Modules:
  0.0 48.4 jit_solution(13871744165279753243)
XLA Ops:
  0.0 1.4 %copy.7.ids_ref = s32[96,2]{1,0:T(8,128)} copy(s32[96,2]{0,1:T(2,128)} %param.7) | data formatting | bytes 1536 | tf_op args[1]
  1.4 1.4 %copy.8.cw_ref = f32[96,2]{1,0:T(8,128)} copy(f32[96,2]{0,1:T(2,128)} %param.8) | data formatting | bytes 1536 | tf_op args[2]
  2.8 44.1 %shard_map.64 = bf16[96,512]{1,0:T(8,128)(2,1)} custom-call(bf16[96,512]{1,0:T(8,128)(2,1)} %x_ref.1, s32[96,2]{1,0:T(8,128)} %copy.7.ids_ref, f32[96,2]{1,0:T(8,128)} %copy.8.cw_ref, bf16[1,896,4096]{2,1,0:T(8,128)(2,1)} %wg_hbm.1, bf16[1,896,4096]{2,1,0:T(8,128)(2,1)} %wu_hbm.1, bf16[1,896,4096]{2,1,0:T(8,128)(2,1)} %wd_hbm.1), custom_call_target="tpu_custom_call" | custom-call | tf_op jit(solution)/shard_map/pallas_call | solution.py:322
  46.9 1.5 %copy.10 = bf16[96,512]{1,0:T(8,128)(2,1)} copy(bf16[96,512]{1,0:T(8,128)(2,1)} %shard_map.64) | data formatting | bytes 196608

commit v2 on v1

--- a/solution.py
+++ b/solution.py
@@ -19,6 +19,12 @@
 def contract_last(left, right):
     return lax.dot_general(
         left, right, (((1,), (1,)), ((), ())), preferred_element_type=jnp.float32
+    )
+
+
+def contract_first(left, right):
+    return lax.dot_general(
+        left, right, (((0,), (0,)), ((), ())), preferred_element_type=jnp.float32
     )
 
 
@@ -102,24 +108,22 @@
         pl.semaphore_signal(barrier, inc=1, device_id=peer, device_id_type=MESH)
 
     ids = ids_ref[...]
-    lanes = lax.broadcasted_iota(jnp.int32, (tokens, 128), 1)
-    first = (ids[:, 0:1] == lanes).astype(jnp.float32)
-    second = (ids[:, 1:2] == lanes).astype(jnp.float32)
+    experts_at = lax.broadcasted_iota(jnp.int32, (8, tokens), 0)
+    first = (ids[0:1] == experts_at).astype(jnp.float32)
+    second = (ids[1:2] == experts_at).astype(jnp.float32)
     earlier = (
-        lax.broadcasted_iota(jnp.int32, (tokens, tokens), 1)
-        < lax.broadcasted_iota(jnp.int32, (tokens, tokens), 0)
+        lax.broadcasted_iota(jnp.int32, (tokens, tokens), 0)
+        < lax.broadcasted_iota(jnp.int32, (tokens, tokens), 1)
     ).astype(jnp.bfloat16)
-    before = jnp.dot(earlier, (first + second).astype(jnp.bfloat16), preferred_element_type=jnp.float32)
-    slot0 = jnp.sum(before * first, axis=1, keepdims=True)
-    slot1 = jnp.sum((before + first) * second, axis=1, keepdims=True)
+    before = jnp.dot((first + second).astype(jnp.bfloat16), earlier, preferred_element_type=jnp.float32)
+    slot0 = jnp.sum(before * first, axis=0, keepdims=True)
+    slot1 = jnp.sum((before + first) * second, axis=0, keepdims=True)
     place = (ids ^ z).astype(jnp.float32) * cap
-    columns = lax.broadcasted_iota(jnp.int32, (tokens, groups * cap), 1).astype(jnp.float32)
-    match0 = (columns == place[:, 0:1] + slot0).astype(jnp.float32)
-    match1 = (columns == place[:, 1:2] + slot1).astype(jnp.float32)
+    slots = lax.broadcasted_iota(jnp.int32, (groups * cap, tokens), 0).astype(jnp.float32)
+    match0 = (slots == place[0:1] + slot0).astype(jnp.float32)
+    match1 = (slots == place[1:2] + slot1).astype(jnp.float32)
     selector = (match0 + match1).astype(jnp.bfloat16)
-    picked[...] = lax.dot_general(
-        selector, x_ref[...], (((0,), (0,)), ((), ())), preferred_element_type=jnp.float32
-    ).astype(jnp.bfloat16)
+    picked[...] = jnp.dot(selector, x_ref[...], preferred_element_type=jnp.float32).astype(jnp.bfloat16)
 
     def group_rows(s):
         return pl.ds(pl.multiple_of(group_of[s] * cap, cap), cap)
@@ -179,19 +183,21 @@
             part = contract_last(rows, weight[:, lanes_at])
             acc[...] = part if start else acc[...] + part
 
-    for s in (3, 2, 1):
+    for s in (1, 2, 3):
         send("z", s, picked.at[pl.ds(s * cap, cap)], block(t, 0), {"expert": group_of[s]})
     share(0)
     arrive("z", 1)
     share(1)
     pass_x(0)
     pass_y(0)
+    pass_x(1)
+    pass_y(1)
     arrive("z", 2)
     share(2)
     arrive("z", 3)
     share(3)
-    pass_x(1)
-    pass_y(1)
+    pass_diag(0)
+    pass_diag(1)
     for load in loads[:4]:
         load.wait()
     for s in steps:
@@ -199,8 +205,6 @@
     project(t, True)
     pass_x(2)
     pass_y(2)
-    pass_diag(0)
-    pass_diag(1)
     pass_x(3)
     pass_y(3)
     for s in steps:
@@ -282,22 +286,21 @@
     sum_x(0)
     sum_y(1)
     arrive("sum_sib", 0)
+    sum_x(1)
+    sum_y(0)
     give_back(2)
     give_back(3)
-    sum_x(1)
-    sum_y(0)
     give_back(1)
     z_in[pl.ds(0, cap)] = total(0)
 
     weights = cw_ref[...]
-    mixing = match0 * weights[:, 0:1] + match1 * weights[:, 1:2]
+    mixing = match0 * weights[0:1] + match1 * weights[1:2]
     coarse = mixing.astype(jnp.bfloat16)
     fine = (mixing - coarse.astype(jnp.float32)).astype(jnp.bfloat16)
     for s in (2, 3, 1):
         arrive("back", s)
     returned = z_in[...]
-    combined = jnp.dot(coarse, returned, preferred_element_type=jnp.float32)
-    combined += jnp.dot(fine, returned, preferred_element_type=jnp.float32)
+    combined = contract_first(coarse, returned) + contract_first(fine, returned)
     out_ref[...] = combined.astype(jnp.bfloat16)
     for copy in copies.values():
         copy.wait_send()
@@ -345,7 +348,7 @@
         compiler_params=pltpu.CompilerParams(
             collective_id=0, has_side_effects=True, vmem_limit_bytes=60 * 1024 * 1024
         ),
-    )(stashed, expert_ids, combine_weight, w_gate, w_up, w_down)
+    )(stashed, expert_ids.T, combine_weight.T, w_gate, w_up, w_down)
 
 
 def picks_kernel(mesh):

time: 48.6 us -> 45.1 us (0.928)
  local copies, waits for them, and re-layouts: 4.32 us -> 1.54 us
  Pallas kernels: 44.1 us -> 43.4 us
    unnamed x3 -> x1, local copies, waits for them, and re-layouts: 4.32 us -> 1.54 us
    pallas_call x1, Pallas kernels: 44.1 us -> 43.4 us  [fused_shards(): pl.pallas_call(functools.partial(layer_kernel, groups, cap), out_shape=ja...]
where the time goes in v2:
time: 45.1 us; the launch traced here: 44.9 us
  Pallas kernels  43.4 us (96%)
  local copies, waits for them, and re-layouts  1.54 us (3%)
    pallas_call x1, Pallas kernels, fused_shards(): pl.pallas_call(functools.partial(layer_kernel, groups, cap), out_shape=ja...  43.4 us
    unnamed x1, local copies, waits for them, and re-layouts  1.54 us

profile of v2, /device:TPU:0, one launch (start us, length us, event | category | flops | bytes accessed | tf_op | source)
XLA Modules:
  0.0 44.9 jit_solution(9271362369926806738)
XLA Ops:
  0.0 43.4 %shard_map.64 = bf16[96,512]{1,0:T(8,128)(2,1)} custom-call(bf16[96,512]{1,0:T(8,128)(2,1)} %x_ref.1, s32[2,96]{1,0:T(2,128)} %bitcast.2, f32[2,96]{1,0:T(2,128)} %bitcast.3, bf16[1,896,4096]{2,1,0:T(8,128)(2,1)} %wg_hbm.1, bf16[1,896,4096]{2,1,0:T(8,128)(2,1)} %wu_hbm.1, bf16[1,896,4096]{2,1,0:T(8,128)(2,1)} %wd_hbm.1), custom_call_target="tpu_custom_call" | custom-call | tf_op jit(solution)/shard_map/pallas_call | solution.py:325
  43.4 1.5 %copy.8 = bf16[96,512]{1,0:T(8,128)(2,1)} copy(bf16[96,512]{1,0:T(8,128)(2,1)} %shard_map.64) | data formatting | bytes 196608
